TPU v7x, 32 devices: a whole 2x2x4 slice. The times are simulated.
32 devices in a mesh: grp: 2 (over y), seq: 8 (over z, x), head: 2 (over core).
Axes of the slice: x: 2, y: 2, z: 4, core: 2. Of those that a mesh axis runs over, the one named last changes fastest.
Arguments:
- key_cache: bfloat16 [4, 64, 128, 1024], P('grp', ('seq', 'head')), parts along dimension 0, may hold values from -160 to 160, as said below
- value_cache: bfloat16 [4, 64, 128, 1024], P('grp', ('seq', 'head')), parts along dimension 0, may hold values from -16 to 16, as said below
- query: bfloat16 [4, 4096], P('grp', 'head'), parts along dimension 0, may hold values from -48 to 48, as said below
- lengths: int32 [4], P('grp'), parts along dimension 0, may hold values from 128 to 8192, as said below
- block_map: int32 [4, 64], P('grp'), parts along dimension 0, may hold values from 0 to 63, each once within a row
Outputs:
- attended: bfloat16 [4, 4096], P('grp', 'head'), parts along dimension 0
There are 2 independent parts, one for each index of `grp`. A program takes and returns all parts, laid end to end along the dimension named above; each array names one. Nothing has to cross between parts.
Inputs may be any that keep to these rules, and one draw needn't show every extreme that they name: `lengths`: every length is a multiple of 128; in every draw some request has length 8192. `key_cache`: finite entries, drawn afresh for every request, block, token and channel. `value_cache`: finite entries, drawn afresh for every request, block, token and channel. `query`: finite entries, drawn afresh for every request, head and channel.
All inputs are finite; a program needn't handle non-finite values.
Results may differ from a plain program's by a relative error of at most 0.0055.
Values may be sent and summed in bfloat16 or wider, within the bound.
A program may use at most 64 MiB of HBM per device.

v0:
```python
import jax
import jax.numpy as jnp
from jax import lax
from jax.sharding import PartitionSpec as P

QH = 32
KVH = 8
HD = 128
BLK = 128


def rescaled(local, top_all):
    factor = jnp.exp(local[0] - top_all)
    return (local[1] * factor, local[2] * factor[..., None])


def partials(key_rows, value_rows, queries, live_blocks):
    batch_rows = key_rows.shape[0]
    slot_count = key_rows.shape[1]
    group_count = key_rows.shape[3] // HD
    token_count = slot_count * BLK
    key_flat = key_rows.reshape(batch_rows, token_count, group_count, HD)
    value_flat = value_rows.reshape(batch_rows, token_count, group_count, HD)
    query_heads = queries.reshape(batch_rows, group_count, QH // KVH, HD)
    logit_scores = jnp.einsum(
        "bgqd,btgd->bgqt", query_heads, key_flat, preferred_element_type=jnp.float32
    )
    logit_scores = logit_scores * (1.0 / HD**0.5)
    logit_scores = logit_scores.reshape(batch_rows, group_count, QH // KVH, slot_count, BLK)
    live_mask = live_blocks[:, None, None, :, None]
    row_top = jnp.max(jnp.where(live_mask, logit_scores, jnp.float32(-1e30)), axis=(3, 4))
    expo = jnp.where(live_mask, jnp.exp(logit_scores - row_top[..., None, None]), jnp.float32(0.0))
    total = jnp.sum(expo, axis=(3, 4))
    weights = expo.astype(jnp.bfloat16).reshape(batch_rows, group_count, QH // KVH, token_count)
    summed_values = jnp.einsum(
        "bgqt,btgd->bgqd", weights, value_flat, preferred_element_type=jnp.float32
    )
    return (row_top, total, summed_values)


def owned_live(block_map, lengths, position, count):
    owned_blocks = lax.dynamic_slice_in_dim(block_map, position * count, count, 1)
    return owned_blocks < (lengths // BLK)[:, None]


def on_device(key_cache, value_cache, query, lengths, block_map):
    batch_rows = key_cache.shape[0]
    width_here = query.shape[1]
    key_rows, value_rows = (
        lax.all_to_all(key_cache, "head", split_axis=3, concat_axis=1, tiled=True),
        lax.all_to_all(value_cache, "head", split_axis=3, concat_axis=1, tiled=True),
    )
    live_blocks = owned_live(block_map, lengths, lax.axis_index("seq"), key_rows.shape[1])
    local = partials(key_rows, value_rows, query, live_blocks)
    top_every = lax.pmax(local[0], "seq")
    total, summed_values = lax.psum(rescaled(local, top_every), "seq")
    result = summed_values / total[..., None]
    return result.reshape(batch_rows, width_here).astype(jnp.bfloat16)


def solution(mesh):
    placed = (
        P("grp", ("seq", "head"), None, None),
        P("grp", ("seq", "head"), None, None),
        P("grp", "head"),
        P("grp"),
        P("grp", None),
    )
    return jax.shard_map(
        on_device, mesh=mesh, in_specs=placed, out_specs=P("grp", "head"), check_vma=False
    )
```

profile of v0, /device:TPU:0, one launch (start us, length us, event | category | flops | bytes accessed | tf_op | source)
XLA Modules:
  0.0 88.1 jit_solution(8158900298736535543)
XLA Ops:
  0.0 4.3 %copy.10 = bf16[2,4,128,1024]{2,1,0,3:T(4,128)(2,1)} copy(bf16[2,4,128,1024]{3,2,1,0:T(8,128)(2,1)} %param.5) | data formatting | bytes 4194304 | tf_op args[0]
  4.3 0.0 copy-start.2
  4.3 0.0 copy-start.1
  4.3 0.0 copy-start
  4.3 3.9 %all-to-all-start = ((bf16[2,4,128,1024]{2,1,0,3:T(4,128)(2,1)}), bf16[2,4,128,1024]{2,1,0,3:T(4,128)(2,1)S(1)}, u32[]{:S(2)}, u32[]{:S(2)}) async-start(bf16[2,4,128,1024]{2,1,0,3:T(4,128)(2,1)} %copy.10), calls=%async_computation | async-start | bytes 4194304 | tf_op jit(solution)/shard_map/all_to_all | solution.py:50
  8.2 0.0 copy-done.2
  8.3 0.0 copy-done.1
  8.3 0.1 dynamic-slice_compare_fusion
  8.3 0.1 broadcast_bitcast_fusion
  8.4 0.0 copy-done
  8.5 4.3 %copy.13 = bf16[2,4,128,1024]{2,1,0,3:T(4,128)(2,1)} copy(bf16[2,4,128,1024]{3,2,1,0:T(8,128)(2,1)} %param.6) | data formatting | bytes 4194304 | tf_op args[1]
  12.8 0.0 all-to-all-done
  12.8 4.8 %all-to-all-start.1 = ((bf16[2,4,128,1024]{2,1,0,3:T(4,128)(2,1)}), bf16[2,4,128,1024]{2,1,0,3:T(4,128)(2,1)}, u32[]{:S(2)}, u32[]{:S(2)}) async-start(bf16[2,4,128,1024]{2,1,0,3:T(4,128)(2,1)} %copy.13), calls=%async_computation.1 | async-start | bytes 4194304 | tf_op jit(solution)/shard_map/all_to_all | solution.py:51
  17.6 3.0 %copy.11 = bf16[2,4,128,2,512]{4,2,1,3,0:T(8,128)(2,1)} copy(bf16[2,4,128,2,512]{2,1,0,4,3:T(4,128)(2,1)S(1)} %bitcast.19) | data formatting | bytes 4194304 | tf_op jit(solution)/shard_map/all_to_all | solution.py:50
  20.6 2.5 %reshape.24 = bf16[2,1024,4,128]{3,2,1,0:T(4,128)(2,1)S(1)} reshape(bf16[2,2,4,128,512]{4,3,2,1,0:T(8,128)(2,1)} %bitcast.20) | data formatting | bytes 4194304 | tf_op jit(solution)/shard_map/reshape | solution.py:22
  23.2 0.7 select_reduce_fusion
  23.9 23.1 %pmax.7 = f32[2,4,4]{2,1,0:T(4,128)S(1)} all-reduce(f32[2,4,4]{2,1,0:T(4,128)S(1)} %get-tuple-element.9), channel_id=1, replica_groups=mesh['grp'=2,'seq'=8,'head'=2] {'seq'}, use_global_device_ids=true, to_apply=%region_1.2 | all-reduce | flops 32 | bytes 256 | tf_op jit(solution)/shard_map/pmax | solution.py:55
  47.0 0.2 fusion.10
  47.3 0.0 all-to-all-done.1
  47.3 3.0 %copy.14 = bf16[2,4,128,2,512]{4,2,1,3,0:T(8,128)(2,1)S(1)} copy(bf16[2,4,128,2,512]{2,1,0,4,3:T(4,128)(2,1)} %bitcast.2) | data formatting | bytes 4194304 | tf_op jit(solution)/shard_map/all_to_all | solution.py:51
  50.2 2.1 %reshape.25 = bf16[2,1024,4,128]{3,2,1,0:T(4,128)(2,1)} reshape(bf16[2,2,4,128,512]{4,3,2,1,0:T(8,128)(2,1)S(1)} %bitcast.21) | data formatting | bytes 4194304 | tf_op jit(solution)/shard_map/reshape | solution.py:23
  52.3 2.0 %fusion.7 = f32[2,4,4,128]{3,2,1,0:T(4,128)S(1)} fusion(bf16[2,1024,4,128]{3,2,1,0:T(4,128)(2,1)} %reshape.25, f32[2,4,4,1024]{3,2,1,0:T(4,128)S(1)} %get-tuple-element.10, f32[2,4,4]{2,1,0:T(4,128)S(1)} %get-tuple-element.9, pred[2,1024]{1,0:T(4,128)(4,1)S(1)} %bitcast.27, f32[2,4,4]{2,1,0:T(4,128)S(1)} %bitcast.29), kind=kOutput, calls=%fused_computation.5 | convolution fusion | flops 8491008 | bytes 2246912 | tf_op jit(solution)/shard_map/bgqt,btgd->bgqd/dot_general | solution.py:35
  54.4 33.0 %all-reduce = (f32[2,4,4,128]{3,2,1,0:T(4,128)S(1)}, f32[2,4,4]{2,1,0:T(4,128)S(1)}) all-reduce(f32[2,4,4,128]{3,2,1,0:T(4,128)S(1)} %fusion.7, f32[2,4,4]{2,1,0:T(4,128)S(1)} %bitcast.24), channel_id=1, replica_groups=mesh['grp'=2,'seq'=8,'head'=2] {'seq'}, use_global_device_ids=true, to_apply=%region_2.3 | all-reduce | flops 4128 | bytes 33024 | tf_op jit(solution)/shard_map/psum | solution.py:56
  87.4 0.1 divide_convert_fusion
  87.5 0.6 convert_element_type.12
  (4 shorter events, 0.0 us)
Async XLA Ops:
  4.3 3.9 %copy-start.2 = (s32[2]{0:T(128)S(1)}, s32[2]{0:T(128)}, u32[]{:S(2)}) copy-start(s32[2]{0:T(128)} %param.8) | copy-start | bytes 28
  4.3 3.9 %copy-start.1 = (s32[2,64]{1,0:T(2,128)S(1)}, s32[2,64]{1,0:T(2,128)}, u32[]{:S(2)}) copy-start(s32[2,64]{1,0:T(2,128)} %param.9) | copy-start | bytes 1540
  4.3 4.1 %copy-start = (bf16[2,2048]{1,0:T(2,128)(2,1)S(1)}, bf16[2,2048]{1,0:T(2,128)(2,1)}, u32[]{:S(2)}) copy-start(bf16[2,2048]{1,0:T(2,128)(2,1)} %param.7) | copy-start | bytes 24580
  4.3 8.5 %all-to-all-start = ((bf16[2,4,128,1024]{2,1,0,3:T(4,128)(2,1)}), bf16[2,4,128,1024]{2,1,0,3:T(4,128)(2,1)S(1)}, u32[]{:S(2)}, u32[]{:S(2)}) async-start(bf16[2,4,128,1024]{2,1,0,3:T(4,128)(2,1)} %copy.10), calls=%async_computation | async-start | bytes 4194304 | tf_op jit(solution)/shard_map/all_to_all | solution.py:50
  12.8 34.5 %all-to-all-start.1 = ((bf16[2,4,128,1024]{2,1,0,3:T(4,128)(2,1)}), bf16[2,4,128,1024]{2,1,0,3:T(4,128)(2,1)}, u32[]{:S(2)}, u32[]{:S(2)}) async-start(bf16[2,4,128,1024]{2,1,0,3:T(4,128)(2,1)} %copy.13), calls=%async_computation.1 | async-start | bytes 4194304 | tf_op jit(solution)/shard_map/all_to_all | solution.py:51
where the time goes:
time: 88.7 us; the launch traced here: 88.1 us
  blocking collectives  56.2 us (63%)
  local copies, waits for them, and re-layouts  20 us (23%)
  starting transfers between devices  8.72 us (10%)
  matrix products  2.79 us (3%)
    psum x1, blocking collectives, on_device(): total, summed_values = lax.psum(rescaled(local, top_every), 'seq')  33 us
    pmax x1, blocking collectives, on_device(): top_every = lax.pmax(local[0], 'seq')  23.1 us
    unnamed x10, local copies, waits for them, and re-layouts  8.71 us
    all_to_all x1, starting transfers between devices, on_device(): lax.all_to_all(value_cache, 'head', split_axis=3, concat_axis=1, tiled=True)  4.82 us
    all_to_all x1, starting transfers between devices, on_device(): lax.all_to_all(key_cache, 'head', split_axis=3, concat_axis=1, tiled=True)  3.9 us
    all_to_all x1, local copies, waits for them, and re-layouts, on_device(): lax.all_to_all(key_cache, 'head', split_axis=3, concat_axis=1, tiled=True)  3.04 us
    all_to_all x1, local copies, waits for them, and re-layouts, on_device(): lax.all_to_all(value_cache, 'head', split_axis=3, concat_axis=1, tiled=True)  2.97 us
    reshape x1, local copies, waits for them, and re-layouts, partials(): key_flat = key_rows.reshape(batch_rows, token_count, group_count, HD)  2.55 us
  transfers between devices with their start and end apart: 2, of which 0 were waited for; matrix products, arithmetic and copies ran while one was open for 13% of the time, Pallas kernels for 0%

commit v1 on v0

v1 whole, which is shorter than its diff:
```python
import functools

import jax
import jax.numpy as jnp
from jax import lax
from jax.experimental import pallas as pl
from jax.experimental.pallas import tpu as pltpu
from jax.sharding import PartitionSpec as P

QH = 32
KVH = 8
HD = 128
BLK = 128
REP = QH // KVH
MESH = pl.DeviceIdType.MESH
NEG = -1e30


def kernel(
    n_seq, n_head,
    lengths, block_map, q_ref, k_hbm, v_hbm, out_ref,
    k_buf, v_buf, q_mate, num_send, stat_send, num_recv, stat_recv,
    kv_sem, q_sem, nsend_sem, nrecv_sem, ssend_sem, srecv_sem,
):
    seq = lax.axis_index("seq")
    head = lax.axis_index("head")
    batch, slots = k_hbm.shape[0], k_hbm.shape[1]
    width = k_hbm.shape[3] // n_head
    groups = width // HD
    rows_b = groups * REP
    rows = batch * rows_b
    tokens = slots * BLK
    me = seq * n_head + head
    n_all = n_seq * n_head
    small = n_all <= 16

    def loop(lo, hi, body):
        if small:
            for i in range(lo, hi):
                body(i)
        else:
            def step(i, carry):
                body(i)
                return carry
            lax.fori_loop(lo, hi, step, 0)

    def peer(step):
        return lax.rem(me + step, n_all)

    def place(device):
        return {"seq": device // n_head, "head": lax.rem(device, n_head)}

    barrier = pltpu.get_barrier_semaphore()

    def greet(step):
        pl.semaphore_signal(barrier, inc=1, device_id=place(peer(step)), device_id_type=MESH)

    loop(1, n_all, greet)

    def load(half, which, b):
        owner = lax.rem(head + half, n_head)
        source, target = ((k_hbm, k_buf), (v_hbm, v_buf))[which]
        lanes = pl.ds(pl.multiple_of(owner * width, width), width)
        return pltpu.make_async_copy(
            source.at[b, :, :, lanes], target.at[half, b], kv_sem.at[half, which, b]
        )

    for half in range(n_head):
        for which in range(2):
            for b in range(batch):
                load(half, which, b).start()

    def live_of(b):
        flags = []
        for j in range(slots):
            here = block_map[b, me * slots + j] * BLK < lengths[b]
            flags.append(jnp.broadcast_to(jnp.where(here, 1.0, 0.0), (rows_b, BLK)))
        return jnp.concatenate(flags, axis=1) > 0.5

    def diagonal(q):
        lifted = q.astype(jnp.float32).reshape(rows, HD)
        wide = jnp.concatenate([lifted] * groups, axis=1)
        row_group = lax.rem(lax.broadcasted_iota(jnp.int32, wide.shape, 0), rows_b) // REP
        lane_group = lax.broadcasted_iota(jnp.int32, wide.shape, 1) // HD
        return jnp.where(row_group == lane_group, wide, 0.0).astype(jnp.bfloat16)

    live = [live_of(b) for b in range(batch)]

    def attend(half, q):
        spread = diagonal(q)
        expos, tops, totals, nums = [], [], [], []
        for b in range(batch):
            load(half, 0, b).wait()
            keys = k_buf[half, b].reshape(tokens, width)
            scores = lax.dot_general(
                spread[b * rows_b:(b + 1) * rows_b], keys, (((1,), (1,)), ((), ())),
                preferred_element_type=jnp.float32,
            ) * (1.0 / HD**0.5)
            scores = jnp.where(live[b], scores, NEG)
            top = jnp.max(scores, axis=1, keepdims=True)
            expo = jnp.where(live[b], jnp.exp(scores - top), 0.0)
            tops.append(top)
            totals.append(jnp.sum(expo, axis=1, keepdims=True))
            expos.append(expo.astype(jnp.bfloat16))
        for b in range(batch):
            load(half, 1, b).wait()
            values = v_buf[half, b].reshape(tokens, width)
            full = jnp.dot(expos[b], values, preferred_element_type=jnp.float32)
            row_group = lax.broadcasted_iota(jnp.int32, (rows_b, HD), 0) // REP
            part = jnp.zeros((rows_b, HD), jnp.float32)
            for g in range(groups):
                part = jnp.where(row_group == g, full[:, g * HD:(g + 1) * HD], part)
            nums.append(part)
        column = jnp.concatenate(tops + totals + [jnp.zeros((HD - 2 * rows, 1), jnp.float32)], axis=0)
        record = jnp.transpose(jnp.broadcast_to(column, (HD, HD)))[0:1]
        return jnp.concatenate(nums, axis=0), record

    def copies(device, half, slot_of):
        return (
            pltpu.make_async_remote_copy(
                src_ref=stat_send.at[pl.ds(half, 1)], dst_ref=stat_recv.at[pl.ds(slot_of, 1)],
                send_sem=ssend_sem.at[device], recv_sem=srecv_sem.at[slot_of],
                device_id=place(device), device_id_type=MESH,
            ),
            pltpu.make_async_remote_copy(
                src_ref=num_send.at[half], dst_ref=num_recv.at[slot_of],
                send_sem=nsend_sem.at[device], recv_sem=nrecv_sem.at[slot_of],
                device_id=place(device), device_id_type=MESH,
            ),
        )

    def send_half(half):
        def one(d):
            target_seq = lax.rem(seq + d, n_seq)
            target = target_seq * n_head + lax.rem(head + half, n_head)
            for copy in copies(target, half, me):
                copy.start()
        loop(0 if half else 1, n_seq, one)

    pl.semaphore_wait(barrier, n_all - 1)
    q_copy = pltpu.make_async_remote_copy(
        src_ref=q_ref, dst_ref=q_mate, send_sem=q_sem.at[0], recv_sem=q_sem.at[1],
        device_id={"head": lax.rem(head + 1, n_head)}, device_id_type=MESH,
    )
    q_copy.start()
    own_num, own_stat = attend(0, q_ref[...])
    num_send[0] = own_num.astype(jnp.bfloat16)
    stat_send[0:1] = own_stat
    send_half(0)
    q_copy.wait()
    mate_num, mate_stat = attend(1, q_mate[...])
    num_send[1] = mate_num.astype(jnp.bfloat16)
    stat_send[1:2] = mate_stat
    send_half(1)

    stat_recv[pl.ds(me, 1)] = own_stat
    num_recv[me] = own_num.astype(jnp.bfloat16)

    def arrive_stat(step):
        copies(peer(step), 0, peer(step))[0].wait_recv()

    def arrive_num(step):
        copies(peer(step), 0, peer(step))[1].wait_recv()

    loop(1, n_all, arrive_stat)
    stats = stat_recv[...]
    top = stats[:, :rows]
    total = stats[:, rows:2 * rows]
    factor = jnp.exp(top - jnp.max(top, axis=0, keepdims=True))
    share = factor / jnp.sum(factor * total, axis=0, keepdims=True)
    share_columns = jnp.transpose(jnp.concatenate(
        [share, jnp.zeros((n_all, HD - rows), jnp.float32)], axis=1))[:rows]
    loop(1, n_all, arrive_num)
    result = jnp.zeros((rows, HD), jnp.float32)
    for s in range(n_all):
        result = result + share_columns[:, s:s + 1] * num_recv[s].astype(jnp.float32)
    out_ref[...] = result.astype(out_ref.dtype)

    def sent(step):
        for copy in copies(peer(step), 0, me):
            copy.wait_send()

    loop(1, n_all, sent)


def solution(mesh):
    n_seq, n_head = mesh.shape["seq"], mesh.shape["head"]
    n_all = n_seq * n_head

    def on_device(key_cache, value_cache, query, lengths, block_map):
        batch, slots, _, channels = key_cache.shape
        width = channels // n_head
        rows = batch * (width // HD) * REP
        dma = pltpu.SemaphoreType.DMA
        result = pl.pallas_call(
            functools.partial(kernel, n_seq, n_head),
            out_shape=jax.ShapeDtypeStruct((rows, HD), jnp.bfloat16),
            in_specs=[
                pl.BlockSpec(memory_space=pltpu.SMEM),
                pl.BlockSpec(memory_space=pltpu.SMEM),
                pl.BlockSpec(memory_space=pltpu.VMEM),
                pl.BlockSpec(memory_space=pl.ANY),
                pl.BlockSpec(memory_space=pl.ANY),
            ],
            out_specs=pl.BlockSpec(memory_space=pltpu.VMEM),
            scratch_shapes=[
                pltpu.VMEM((n_head, batch, slots, BLK, width), jnp.bfloat16),
                pltpu.VMEM((n_head, batch, slots, BLK, width), jnp.bfloat16),
                pltpu.VMEM(query.shape, jnp.bfloat16),
                pltpu.VMEM((n_head, rows, HD), jnp.bfloat16),
                pltpu.VMEM((n_head, HD), jnp.float32),
                pltpu.VMEM((n_all, rows, HD), jnp.bfloat16),
                pltpu.VMEM((n_all, HD), jnp.float32),
                dma((n_head, 2, batch)),
                dma((2,)),
                dma((n_all,)),
                dma((n_all,)),
                dma((n_all,)),
                dma((n_all,)),
            ],
            compiler_params=pltpu.CompilerParams(collective_id=0, has_side_effects=True),
        )(lengths, block_map, query, key_cache, value_cache)
        return result.reshape(query.shape)

    placed = (
        P("grp", ("seq", "head"), None, None),
        P("grp", ("seq", "head"), None, None),
        P("grp", "head"),
        P("grp"),
        P("grp", None),
    )
    return jax.shard_map(
        on_device, mesh=mesh, in_specs=placed, out_specs=P("grp", "head"), check_vma=False
    )
```

time: 88.7 us -> 14.9 us (0.17)
  blocking collectives: 56.2 us -> 0 us
  local copies, waits for them, and re-layouts: 20 us -> 1.31 us
  Pallas kernels: 0 us -> 13.4 us
  starting transfers between devices: 8.72 us -> 0 us
  matrix products: 2.79 us -> 0 us
    psum x1 -> x0, blocking collectives: 33 us -> none  [on_device(): total, summed_values = lax.psum(rescaled(local, top_every), 'seq')]
    pmax x1 -> x0, blocking collectives: 23.1 us -> none  [on_device(): top_every = lax.pmax(local[0], 'seq')]
    pallas_call x0 -> x1, Pallas kernels: none -> 13.4 us  [on_device(): pl.pallas_call(functools.partial(kernel, n_seq, n_head), out_shape=jax.Sh...]
    all_to_all x2 -> x0, starting transfers between devices: 8.72 us -> none  [the longest x1 4.82 us: on_device(): lax.all_to_all(value_cache, 'head', split_axis=3, concat_axis=1, tiled=True)]
    unnamed x10 -> x0, local copies, waits for them, and re-layouts: 8.71 us -> none
    all_to_all x2 -> x0, local copies, waits for them, and re-layouts: 6.01 us -> none  [the longest x1 3.04 us: on_device(): lax.all_to_all(key_cache, 'head', split_axis=3, concat_axis=1, tiled=True)]
    reshape x3 -> x1, local copies, waits for them, and re-layouts: 4.65 us -> 1.31 us  [on_device(): return result.reshape(query.shape)]
    dot_general x2 -> x0, matrix products: 2.79 us -> none  [the longest x1 2.05 us: partials(): jnp.einsum('bgqt,btgd->bgqd', weights, value_flat, preferred_element_type...]
  transfers between devices with their start and end apart: 2 -> 0, of which waited for: 0 -> 0; matrix products, arithmetic and copies ran while one was open for 13% -> 0% of each run, Pallas kernels for 0% -> 0%
where the time goes in v1:
time: 14.9 us; the launch traced here: 14.7 us
  Pallas kernels  13.4 us (90%)
  local copies, waits for them, and re-layouts  1.31 us (9%)
    pallas_call x1, Pallas kernels, on_device(): pl.pallas_call(functools.partial(kernel, n_seq, n_head), out_shape=jax.Sh...  13.4 us
    reshape x1, local copies, waits for them, and re-layouts, on_device(): return result.reshape(query.shape)  1.31 us

profile of v1, /device:TPU:0, one launch (start us, length us, event | category | flops | bytes accessed | tf_op | source)
XLA Modules:
  0.0 14.7 jit_solution(11918299982254342528)
XLA Ops:
  0.0 13.4 %shard_map.55 = bf16[32,128]{1,0:T(8,128)(2,1)} custom-call(s32[2]{0:T(128)} %lengths.1, s32[2,64]{1,0:T(2,128)} %block_map.1, bf16[2,2048]{1,0:T(2,128)(2,1)} %q_ref.1, bf16[2,4,128,1024]{3,2,1,0:T(8,128)(2,1)} %k_hbm.1, bf16[2,4,128,1024]{3,2,1,0:T(8,128)(2,1)} %v_hbm.1), custom_call_target="tpu_custom_call" | custom-call | tf_op jit(solution)/shard_map/pallas_call | solution.py:195
  13.4 1.3 %reshape.3 = bf16[2,2048]{1,0:T(2,128)(2,1)} reshape(bf16[32,128]{1,0:T(8,128)(2,1)} %shard_map.55) | data formatting | bytes 16384 | tf_op jit(solution)/shard_map/reshape | solution.py:223

commit v2 on v1

v2 whole, which is shorter than its diff:
```python
import functools

import jax
import jax.numpy as jnp
from jax import lax
from jax.experimental import pallas as pl
from jax.experimental.pallas import tpu as pltpu
from jax.sharding import PartitionSpec as P

QH = 32
KVH = 8
HD = 128
BLK = 128
REP = QH // KVH
MESH = pl.DeviceIdType.MESH
NEG = -1e30


def kernel(
    n_seq, n_head, n_plane,
    lengths_hbm, map_hbm, q_hbm, k_hbm, v_hbm, out_ref,
    lengths, block_map, q_own, q_mate, k_buf, v_buf,
    num_send, stat_send, num_recv, stat_recv, num_send2, stat_send2, num_recv2, stat_recv2,
    small_sem, q_sem, kv_sem, num_sem, stat_sem, num_sem2, stat_sem2, up_sem, down_sem,
):
    seq = lax.axis_index("seq")
    head = lax.axis_index("head")
    batch, slots = k_hbm.shape[0], k_hbm.shape[1]
    width = k_hbm.shape[3] // n_head
    groups = width // HD
    rows_b = groups * REP
    rows = batch * rows_b
    tokens = slots * BLK
    n_line = n_seq // n_plane
    line, across = seq // n_plane, lax.rem(seq, n_plane)
    members = n_plane * n_head
    spot = across * n_head + head
    me = seq * n_head + head

    barrier = pltpu.get_barrier_semaphore()
    below, above = line > 0, line < n_line - 1

    def signal(sem, device):
        pl.semaphore_signal(sem, inc=1, device_id=device, device_id_type=MESH)

    @pl.when(below)
    def _():
        signal(barrier, {"seq": seq - n_plane})

    @pl.when(above)
    def _():
        signal(barrier, {"seq": seq + n_plane})

    for step in range(1, members):
        other = lax.rem(spot + step, members)
        signal(barrier, {"seq": line * n_plane + other // n_head, "head": lax.rem(other, n_head)})

    q_load = pltpu.make_async_copy(q_hbm, q_own, small_sem.at[0])
    q_load.start()
    length_load = pltpu.make_async_copy(lengths_hbm, lengths, small_sem.at[1])
    length_load.start()
    map_load = pltpu.make_async_copy(map_hbm, block_map, small_sem.at[2])
    map_load.start()

    def load(half, which, b):
        owner = lax.rem(head + half, n_head)
        source, target = ((k_hbm, k_buf), (v_hbm, v_buf))[which]
        lanes = pl.ds(pl.multiple_of(owner * width, width), width)
        return pltpu.make_async_copy(
            source.at[b, :, :, lanes], target.at[half, b], kv_sem.at[half, which, b]
        )

    for half in range(n_head):
        for which in range(2):
            for b in range(batch):
                load(half, which, b).start()

    length_load.wait()
    map_load.wait()
    q_load.wait()
    contacts = members - 1 + below.astype(jnp.int32) + above.astype(jnp.int32)
    pl.semaphore_wait(barrier, contacts)
    q_copy = pltpu.make_async_remote_copy(
        src_ref=q_own, dst_ref=q_mate, send_sem=q_sem.at[0], recv_sem=q_sem.at[1],
        device_id={"head": lax.rem(head + 1, n_head)}, device_id_type=MESH,
    )
    q_copy.start()

    @pl.when(above)
    def _():
        signal(up_sem, {"seq": seq + n_plane})

    @pl.when(below)
    def _():
        signal(down_sem, {"seq": seq - n_plane})

    def relay(lo, hi):
        for step in range(lo, hi):
            @pl.when(line >= step)
            def _():
                pl.semaphore_wait(up_sem, 1)

            @pl.when((line >= step) & above)
            def _():
                signal(up_sem, {"seq": seq + n_plane})

            @pl.when(n_line - 1 - line >= step)
            def _():
                pl.semaphore_wait(down_sem, 1)

            @pl.when((n_line - 1 - line >= step) & below)
            def _():
                signal(down_sem, {"seq": seq - n_plane})

    def live_of(b):
        flags = []
        for j in range(slots):
            here = block_map[b, me * slots + j] * BLK < lengths[b]
            flags.append(jnp.broadcast_to(jnp.where(here, 1.0, 0.0), (rows_b, BLK)))
        return jnp.concatenate(flags, axis=1) > 0.5

    def diagonal(q):
        lifted = q.astype(jnp.float32).reshape(rows, HD)
        wide = jnp.concatenate([lifted] * groups, axis=1)
        row_group = lax.rem(lax.broadcasted_iota(jnp.int32, wide.shape, 0), rows_b) // REP
        lane_group = lax.broadcasted_iota(jnp.int32, wide.shape, 1) // HD
        return jnp.where(row_group == lane_group, wide, 0.0).astype(jnp.bfloat16)

    live = [live_of(b) for b in range(batch)]

    def attend(half, q):
        spread = diagonal(q)
        expos, tops, totals, nums = [], [], [], []
        for b in range(batch):
            load(half, 0, b).wait()
            keys = k_buf[half, b].reshape(tokens, width)
            scores = lax.dot_general(
                spread[b * rows_b:(b + 1) * rows_b], keys, (((1,), (1,)), ((), ())),
                preferred_element_type=jnp.float32,
            ) * (1.0 / HD**0.5)
            scores = jnp.where(live[b], scores, NEG)
            top = jnp.max(scores, axis=1, keepdims=True)
            expo = jnp.where(live[b], jnp.exp(scores - top), 0.0)
            tops.append(top)
            totals.append(jnp.sum(expo, axis=1, keepdims=True))
            expos.append(expo.astype(jnp.bfloat16))
        for b in range(batch):
            load(half, 1, b).wait()
            values = v_buf[half, b].reshape(tokens, width)
            full = jnp.dot(expos[b], values, preferred_element_type=jnp.float32)
            row_group = lax.broadcasted_iota(jnp.int32, (rows_b, HD), 0) // REP
            part = jnp.zeros((rows_b, HD), jnp.float32)
            for g in range(groups):
                part = jnp.where(row_group == g, full[:, g * HD:(g + 1) * HD], part)
            nums.append(part)
        column = jnp.concatenate(tops + totals + [jnp.zeros((HD - 2 * rows, 1), jnp.float32)], axis=0)
        record = jnp.transpose(jnp.broadcast_to(column, (HD, HD)))[0:1]
        return jnp.concatenate(nums, axis=0), record

    def hand(source, target, sems, index, slot, device):
        return pltpu.make_async_remote_copy(
            src_ref=source, dst_ref=target, send_sem=sems.at[0, index], recv_sem=sems.at[1, slot],
            device_id=device, device_id_type=MESH,
        )

    def plane_hand(kind, half, other, slot):
        device = {"seq": line * n_plane + other // n_head, "head": lax.rem(other, n_head)}
        if kind == 0:
            return hand(stat_send.at[pl.ds(half, 1)], stat_recv.at[pl.ds(slot, 1)], stat_sem, other, slot, device)
        return hand(num_send.at[half], num_recv.at[slot], num_sem, other, slot, device)

    def line_hand(kind, other, slot):
        device = {"seq": other * n_plane + across}
        if kind == 0:
            return hand(stat_send2, stat_recv2.at[pl.ds(slot, 1)], stat_sem2, other, slot, device)
        return hand(num_send2, num_recv2.at[slot], num_sem2, other, slot, device)

    def plane_send(half):
        for kind in range(2):
            for d in range(0 if half else 1, n_plane):
                other = lax.rem(across + d, n_plane) * n_head + lax.rem(head + half, n_head)
                plane_hand(kind, half, other, spot).start()

    def merged(stats):
        top, total = stats[:, :rows], stats[:, rows:2 * rows]
        best = jnp.max(top, axis=0, keepdims=True)
        factor = jnp.exp(top - best)
        whole = jnp.sum(factor * total, axis=0, keepdims=True)
        return best, factor, whole

    def columns(factor):
        count = factor.shape[0]
        padded = -count % 8
        tall = factor if not padded else jnp.concatenate(
            [factor, jnp.zeros((padded, rows), jnp.float32)], axis=0)
        return jnp.transpose(jnp.concatenate(
            [tall, jnp.zeros((tall.shape[0], HD - rows), jnp.float32)], axis=1))[:rows]

    own_num, own_stat = attend(0, q_own[...])
    num_send[0] = own_num.astype(jnp.bfloat16)
    stat_send[0:1] = own_stat
    plane_send(0)
    relay(1, 2)
    q_copy.wait()
    mate_num, mate_stat = attend(1, q_mate[...])
    num_send[1] = mate_num.astype(jnp.bfloat16)
    stat_send[1:2] = mate_stat
    plane_send(1)
    relay(2, n_line)

    stat_recv[pl.ds(spot, 1)] = own_stat
    num_recv[spot] = own_num.astype(jnp.bfloat16)
    for kind in range(2):
        for step in range(1, members):
            other = lax.rem(spot + step, members)
            plane_hand(kind, 0, other, other).wait_recv()
    best, factor, whole = merged(stat_recv[...])
    share = columns(factor)
    plane_num = jnp.zeros((rows, HD), jnp.float32)
    for s in range(members):
        plane_num = plane_num + share[:, s:s + 1] * num_recv[s].astype(jnp.float32)
    plane_stat = jnp.concatenate(
        [best, whole, jnp.zeros((1, HD - 2 * rows), jnp.float32)], axis=1)
    stat_send2[...] = plane_stat
    num_send2[...] = plane_num.astype(jnp.bfloat16)
    for kind in range(2):
        for step in range(1, n_line):
            line_hand(kind, lax.rem(line + step, n_line), line).start()
    stat_recv2[pl.ds(line, 1)] = plane_stat
    num_recv2[line] = plane_num.astype(jnp.bfloat16)
    for kind in range(2):
        for step in range(1, n_line):
            other = lax.rem(line + step, n_line)
            line_hand(kind, other, other).wait_recv()
    best, factor, whole = merged(stat_recv2[...])
    share = columns(factor / whole)
    result = jnp.zeros((rows, HD), jnp.float32)
    for s in range(n_line):
        result = result + share[:, s:s + 1] * num_recv2[s].astype(jnp.float32)
    out_ref[...] = result.reshape(batch, rows_b * HD).astype(out_ref.dtype)

    for kind in range(2):
        for step in range(1, members):
            other = lax.rem(spot + step, members)
            plane_hand(kind, 0, other, spot).wait_send()
        for step in range(1, n_line):
            line_hand(kind, lax.rem(line + step, n_line), line).wait_send()


def plane_of(n_seq):
    size = 1
    while (size + 1) ** 2 <= n_seq:
        size += 1
    while n_seq % size:
        size -= 1
    return size


def solution(mesh):
    n_seq, n_head = mesh.shape["seq"], mesh.shape["head"]
    n_plane = plane_of(n_seq)
    n_line, members = n_seq // n_plane, n_plane * n_head

    def on_device(key_cache, value_cache, query, lengths, block_map):
        batch, slots, _, channels = key_cache.shape
        width = channels // n_head
        rows = batch * (width // HD) * REP
        dma = pltpu.SemaphoreType.DMA
        result = pl.pallas_call(
            functools.partial(kernel, n_seq, n_head, n_plane),
            out_shape=jax.ShapeDtypeStruct(query.shape, jnp.bfloat16),
            in_specs=[pl.BlockSpec(memory_space=pl.ANY)] * 5,
            out_specs=pl.BlockSpec(memory_space=pltpu.VMEM),
            scratch_shapes=[
                pltpu.SMEM(lengths.shape, jnp.int32),
                pltpu.SMEM(block_map.shape, jnp.int32),
                pltpu.VMEM(query.shape, jnp.bfloat16),
                pltpu.VMEM(query.shape, jnp.bfloat16),
                pltpu.VMEM((n_head, batch, slots, BLK, width), jnp.bfloat16),
                pltpu.VMEM((n_head, batch, slots, BLK, width), jnp.bfloat16),
                pltpu.VMEM((n_head, rows, HD), jnp.bfloat16),
                pltpu.VMEM((n_head, HD), jnp.float32),
                pltpu.VMEM((members, rows, HD), jnp.bfloat16),
                pltpu.VMEM((members, HD), jnp.float32),
                pltpu.VMEM((rows, HD), jnp.bfloat16),
                pltpu.VMEM((1, HD), jnp.float32),
                pltpu.VMEM((n_line, rows, HD), jnp.bfloat16),
                pltpu.VMEM((n_line, HD), jnp.float32),
                dma((3,)),
                dma((2,)),
                dma((n_head, 2, batch)),
                dma((2, members)),
                dma((2, members)),
                dma((2, n_line)),
                dma((2, n_line)),
                pltpu.SemaphoreType.REGULAR,
                pltpu.SemaphoreType.REGULAR,
            ],
            compiler_params=pltpu.CompilerParams(collective_id=0, has_side_effects=True),
        )(lengths, block_map, query, key_cache, value_cache)
        return result

    placed = (
        P("grp", ("seq", "head"), None, None),
        P("grp", ("seq", "head"), None, None),
        P("grp", "head"),
        P("grp"),
        P("grp", None),
    )
    return jax.shard_map(
        on_device, mesh=mesh, in_specs=placed, out_specs=P("grp", "head"), check_vma=False
    )
```

time: 14.9 us -> 16.2 us (1.087)
  Pallas kernels: 13.4 us -> 14.7 us
    pallas_call x1, Pallas kernels: 13.4 us -> 14.7 us  [on_device(): pl.pallas_call(functools.partial(kernel, n_seq, n_head, n_plane), out_sha...]
    reshape x1 -> x0, local copies, waits for them, and re-layouts: 1.31 us -> none  [on_device(): return result.reshape(query.shape)]
    unnamed x0 -> x1, local copies, waits for them, and re-layouts: none -> 1.3 us
where the time goes in v2:
time: 16.2 us; the launch traced here: 16 us
  Pallas kernels  14.7 us (91%)
  local copies, waits for them, and re-layouts  1.3 us (8%)
    pallas_call x1, Pallas kernels, on_device(): pl.pallas_call(functools.partial(kernel, n_seq, n_head, n_plane), out_sha...  14.7 us
    unnamed x1, local copies, waits for them, and re-layouts  1.3 us

profile of v2, /device:TPU:0, one launch (start us, length us, event | category | flops | bytes accessed | tf_op | source)
XLA Modules:
  0.0 16.0 jit_solution(72232577433134933)
XLA Ops:
  0.0 14.7 %shard_map.55 = bf16[2,2048]{1,0:T(2,128)(2,1)} custom-call(s32[2]{0:T(128)} %lengths_hbm.1, s32[2,64]{1,0:T(2,128)} %map_hbm.1, bf16[2,2048]{1,0:T(2,128)(2,1)} %q_hbm.1, bf16[2,4,128,1024]{3,2,1,0:T(8,128)(2,1)} %k_hbm.1, bf16[2,4,128,1024]{3,2,1,0:T(8,128)(2,1)} %v_hbm.1), custom_call_target="tpu_custom_call" | custom-call | tf_op jit(solution)/shard_map/pallas_call | solution.py:269
  14.7 1.3 %copy.7 = bf16[2,2048]{1,0:T(2,128)(2,1)} copy(bf16[2,2048]{1,0:T(2,128)(2,1)} %shard_map.55) | data formatting | bytes 16384

commit v3 on v1

--- a/solution.py
+++ b/solution.py
@@ -18,7 +18,8 @@
 
 def kernel(
     n_seq, n_head,
-    lengths, block_map, q_ref, k_hbm, v_hbm, out_ref,
+    lengths_hbm, map_hbm, q_hbm, k_hbm, v_hbm, out_ref,
+    lengths, block_map, q_ref, small_sem,
     k_buf, v_buf, q_mate, num_send, stat_send, num_recv, stat_recv,
     kv_sem, q_sem, nsend_sem, nrecv_sem, ssend_sem, srecv_sem,
 ):
@@ -56,6 +57,10 @@
         pl.semaphore_signal(barrier, inc=1, device_id=place(peer(step)), device_id_type=MESH)
 
     loop(1, n_all, greet)
+    smalls = [pltpu.make_async_copy(a, b, small_sem.at[i]) for i, (a, b) in enumerate(
+        ((q_hbm, q_ref), (lengths_hbm, lengths), (map_hbm, block_map)))]
+    for copy in smalls:
+        copy.start()
 
     def load(half, which, b):
         owner = lax.rem(head + half, n_head)
@@ -84,6 +89,8 @@
         lane_group = lax.broadcasted_iota(jnp.int32, wide.shape, 1) // HD
         return jnp.where(row_group == lane_group, wide, 0.0).astype(jnp.bfloat16)
 
+    for copy in smalls:
+        copy.wait()
     live = [live_of(b) for b in range(batch)]
 
     def attend(half, q):
@@ -174,7 +181,7 @@
     result = jnp.zeros((rows, HD), jnp.float32)
     for s in range(n_all):
         result = result + share_columns[:, s:s + 1] * num_recv[s].astype(jnp.float32)
-    out_ref[...] = result.astype(out_ref.dtype)
+    out_ref[...] = result.reshape(batch, rows_b * HD).astype(out_ref.dtype)
 
     def sent(step):
         for copy in copies(peer(step), 0, me):
@@ -194,16 +201,16 @@
         dma = pltpu.SemaphoreType.DMA
         result = pl.pallas_call(
             functools.partial(kernel, n_seq, n_head),
-            out_shape=jax.ShapeDtypeStruct((rows, HD), jnp.bfloat16),
+            out_shape=pltpu.VMEM(query.shape, jnp.bfloat16),
             in_specs=[
-                pl.BlockSpec(memory_space=pltpu.SMEM),
-                pl.BlockSpec(memory_space=pltpu.SMEM),
-                pl.BlockSpec(memory_space=pltpu.VMEM),
-                pl.BlockSpec(memory_space=pl.ANY),
-                pl.BlockSpec(memory_space=pl.ANY),
+                *[pl.BlockSpec(memory_space=pl.ANY)] * 5,
             ],
             out_specs=pl.BlockSpec(memory_space=pltpu.VMEM),
             scratch_shapes=[
+                pltpu.SMEM(lengths.shape, jnp.int32),
+                pltpu.SMEM(block_map.shape, jnp.int32),
+                pltpu.VMEM(query.shape, jnp.bfloat16),
+                dma((3,)),
                 pltpu.VMEM((n_head, batch, slots, BLK, width), jnp.bfloat16),
                 pltpu.VMEM((n_head, batch, slots, BLK, width), jnp.bfloat16),
                 pltpu.VMEM(query.shape, jnp.bfloat16),
@@ -220,7 +227,7 @@
             ],
             compiler_params=pltpu.CompilerParams(collective_id=0, has_side_effects=True),
         )(lengths, block_map, query, key_cache, value_cache)
-        return result.reshape(query.shape)
+        return result
 
     placed = (
         P("grp", ("seq", "head"), None, None),

time: 14.9 us -> 12.8 us (0.86)
  Pallas kernels: 13.4 us -> 12.1 us
  local copies, waits for them, and re-layouts: 1.31 us -> 0.6 us
    reshape x1 -> x0, local copies, waits for them, and re-layouts: 1.31 us -> none  [on_device(): return result.reshape(query.shape)]
    pallas_call x1, Pallas kernels: 13.4 us -> 12.1 us  [on_device(): pl.pallas_call(functools.partial(kernel, n_seq, n_head), out_shape=pltpu....]
    unnamed x0 -> x1, local copies, waits for them, and re-layouts: none -> 0.6 us
where the time goes in v3:
time: 12.8 us; the launch traced here: 12.7 us
  Pallas kernels  12.1 us (95%)
  local copies, waits for them, and re-layouts  0.6 us (5%)
    pallas_call x1, Pallas kernels, on_device(): pl.pallas_call(functools.partial(kernel, n_seq, n_head), out_shape=pltpu....  12.1 us
    unnamed x1, local copies, waits for them, and re-layouts  0.6 us

profile of v3, /device:TPU:0, one launch (start us, length us, event | category | flops | bytes accessed | tf_op | source)
XLA Modules:
  0.0 12.7 jit_solution(16723741938353107822)
XLA Ops:
  0.0 12.1 %shard_map.55 = bf16[2,2048]{1,0:T(2,128)(2,1)S(1)} custom-call(s32[2]{0:T(128)} %lengths_hbm.1, s32[2,64]{1,0:T(2,128)} %map_hbm.1, bf16[2,2048]{1,0:T(2,128)(2,1)} %q_hbm.1, bf16[2,4,128,1024]{3,2,1,0:T(8,128)(2,1)} %k_hbm.1, bf16[2,4,128,1024]{3,2,1,0:T(8,128)(2,1)} %v_hbm.1), custom_call_target="tpu_custom_call" | custom-call | tf_op jit(solution)/shard_map/pallas_call | solution.py:202
  12.1 0.6 %copy.7 = bf16[2,2048]{1,0:T(2,128)(2,1)} copy(bf16[2,2048]{1,0:T(2,128)(2,1)S(1)} %shard_map.55) | data formatting | bytes 16384

commit v4 on v3

--- a/solution.py
+++ b/solution.py
@@ -98,6 +98,7 @@
         expos, tops, totals, nums = [], [], [], []
         for b in range(batch):
             load(half, 0, b).wait()
+        for b in range(batch):
             keys = k_buf[half, b].reshape(tokens, width)
             scores = lax.dot_general(
                 spread[b * rows_b:(b + 1) * rows_b], keys, (((1,), (1,)), ((), ())),
@@ -111,6 +112,7 @@
             expos.append(expo.astype(jnp.bfloat16))
         for b in range(batch):
             load(half, 1, b).wait()
+        for b in range(batch):
             values = v_buf[half, b].reshape(tokens, width)
             full = jnp.dot(expos[b], values, preferred_element_type=jnp.float32)
             row_group = lax.broadcasted_iota(jnp.int32, (rows_b, HD), 0) // REP

time: 12.8 us -> 12.3 us (0.961)
  Pallas kernels: 12.1 us -> 11.6 us
    pallas_call x1, Pallas kernels: 12.1 us -> 11.6 us  [on_device(): pl.pallas_call(functools.partial(kernel, n_seq, n_head), out_shape=pltpu....]
where the time goes in v4:
time: 12.3 us; the launch traced here: 12.2 us
  Pallas kernels  11.6 us (94%)
  local copies, waits for them, and re-layouts  0.6 us (5%)
    pallas_call x1, Pallas kernels, on_device(): pl.pallas_call(functools.partial(kernel, n_seq, n_head), out_shape=pltpu....  11.6 us
    unnamed x1, local copies, waits for them, and re-layouts  0.6 us

profile of v4, /device:TPU:0, one launch (start us, length us, event | category | flops | bytes accessed | tf_op | source)
XLA Modules:
  0.0 12.2 jit_solution(6978606552698545273)
XLA Ops:
  0.0 11.6 %shard_map.55 = bf16[2,2048]{1,0:T(2,128)(2,1)S(1)} custom-call(s32[2]{0:T(128)} %lengths_hbm.1, s32[2,64]{1,0:T(2,128)} %map_hbm.1, bf16[2,2048]{1,0:T(2,128)(2,1)} %q_hbm.1, bf16[2,4,128,1024]{3,2,1,0:T(8,128)(2,1)} %k_hbm.1, bf16[2,4,128,1024]{3,2,1,0:T(8,128)(2,1)} %v_hbm.1), custom_call_target="tpu_custom_call" | custom-call | tf_op jit(solution)/shard_map/pallas_call | solution.py:204
  11.6 0.6 %copy.7 = bf16[2,2048]{1,0:T(2,128)(2,1)} copy(bf16[2,2048]{1,0:T(2,128)(2,1)S(1)} %shard_map.55) | data formatting | bytes 16384

commit v5 on v4

--- a/solution.py
+++ b/solution.py
@@ -56,12 +56,11 @@
     def greet(step):
         pl.semaphore_signal(barrier, inc=1, device_id=place(peer(step)), device_id_type=MESH)
 
-    loop(1, n_all, greet)
     smalls = [pltpu.make_async_copy(a, b, small_sem.at[i]) for i, (a, b) in enumerate(
         ((q_hbm, q_ref), (lengths_hbm, lengths), (map_hbm, block_map)))]
     for copy in smalls:
         copy.start()
-
+    loop(1, n_all, greet)
     def load(half, which, b):
         owner = lax.rem(head + half, n_head)
         source, target = ((k_hbm, k_buf), (v_hbm, v_buf))[which]

time: 12.3 us -> 12.4 us (level)
  no operation moved by 1% of the time
where the time goes in v5:
time: 12.4 us; the launch traced here: 12.2 us
  Pallas kernels  11.6 us (94%)
  local copies, waits for them, and re-layouts  0.6 us (5%)
    pallas_call x1, Pallas kernels, on_device(): pl.pallas_call(functools.partial(kernel, n_seq, n_head), out_shape=pltpu....  11.6 us
    unnamed x1, local copies, waits for them, and re-layouts  0.6 us

profile of v5, /device:TPU:0, one launch (start us, length us, event | category | flops | bytes accessed | tf_op | source)
XLA Modules:
  0.0 12.2 jit_solution(1283811273414504451)
XLA Ops:
  0.0 11.6 %shard_map.55 = bf16[2,2048]{1,0:T(2,128)(2,1)S(1)} custom-call(s32[2]{0:T(128)} %lengths_hbm.1, s32[2,64]{1,0:T(2,128)} %map_hbm.1, bf16[2,2048]{1,0:T(2,128)(2,1)} %q_hbm.1, bf16[2,4,128,1024]{3,2,1,0:T(8,128)(2,1)} %k_hbm.1, bf16[2,4,128,1024]{3,2,1,0:T(8,128)(2,1)} %v_hbm.1), custom_call_target="tpu_custom_call" | custom-call | tf_op jit(solution)/shard_map/pallas_call | solution.py:203
  11.6 0.6 %copy.7 = bf16[2,2048]{1,0:T(2,128)(2,1)} copy(bf16[2,2048]{1,0:T(2,128)(2,1)S(1)} %shard_map.55) | data formatting | bytes 16384

commit v6 on v5

--- a/solution.py
+++ b/solution.py
@@ -95,8 +95,9 @@
     def attend(half, q):
         spread = diagonal(q)
         expos, tops, totals, nums = [], [], [], []
-        for b in range(batch):
-            load(half, 0, b).wait()
+        if half == 0:
+            for b in range(batch):
+                load(half, 0, b).wait()
         for b in range(batch):
             keys = k_buf[half, b].reshape(tokens, width)
             scores = lax.dot_general(
@@ -111,6 +112,8 @@
             expos.append(expo.astype(jnp.bfloat16))
         for b in range(batch):
             load(half, 1, b).wait()
+            if half == 0:
+                load(1, 0, b).wait()
         for b in range(batch):
             values = v_buf[half, b].reshape(tokens, width)
             full = jnp.dot(expos[b], values, preferred_element_type=jnp.float32)
@@ -119,8 +122,9 @@
             for g in range(groups):
                 part = jnp.where(row_group == g, full[:, g * HD:(g + 1) * HD], part)
             nums.append(part)
-        column = jnp.concatenate(tops + totals + [jnp.zeros((HD - 2 * rows, 1), jnp.float32)], axis=0)
-        record = jnp.transpose(jnp.broadcast_to(column, (HD, HD)))[0:1]
+        column = jnp.concatenate(tops + totals, axis=0)
+        record = jnp.transpose(jnp.broadcast_to(column, (2 * rows, HD)))[0:1]
+        record = jnp.concatenate([record, jnp.zeros((1, HD - 2 * rows), jnp.float32)], axis=1)
         return jnp.concatenate(nums, axis=0), record
 
     def copies(device, half, slot_of):
@@ -179,9 +183,10 @@
     share_columns = jnp.transpose(jnp.concatenate(
         [share, jnp.zeros((n_all, HD - rows), jnp.float32)], axis=1))[:rows]
     loop(1, n_all, arrive_num)
-    result = jnp.zeros((rows, HD), jnp.float32)
-    for s in range(n_all):
-        result = result + share_columns[:, s:s + 1] * num_recv[s].astype(jnp.float32)
+    terms = [share_columns[:, s:s + 1] * num_recv[s].astype(jnp.float32) for s in range(n_all)]
+    while len(terms) > 1:
+        terms = [sum(terms[i + 1:i + 2], terms[i]) for i in range(0, len(terms), 2)]
+    result = terms[0]
     out_ref[...] = result.reshape(batch, rows_b * HD).astype(out_ref.dtype)
 
     def sent(step):

time: 12.4 us -> 12.4 us (level)
  no operation moved by 1% of the time
where the time goes in v6:
time: 12.4 us; the launch traced here: 12.2 us
  Pallas kernels  11.6 us (94%)
  local copies, waits for them, and re-layouts  0.6 us (5%)
    pallas_call x1, Pallas kernels, on_device(): pl.pallas_call(functools.partial(kernel, n_seq, n_head), out_shape=pltpu....  11.6 us
    unnamed x1, local copies, waits for them, and re-layouts  0.6 us

profile of v6, /device:TPU:0, one launch (start us, length us, event | category | flops | bytes accessed | tf_op | source)
XLA Modules:
  0.0 12.2 jit_solution(8320412115162061176)
XLA Ops:
  0.0 11.6 %shard_map.55 = bf16[2,2048]{1,0:T(2,128)(2,1)S(1)} custom-call(s32[2]{0:T(128)} %lengths_hbm.1, s32[2,64]{1,0:T(2,128)} %map_hbm.1, bf16[2,2048]{1,0:T(2,128)(2,1)} %q_hbm.1, bf16[2,4,128,1024]{3,2,1,0:T(8,128)(2,1)} %k_hbm.1, bf16[2,4,128,1024]{3,2,1,0:T(8,128)(2,1)} %v_hbm.1), custom_call_target="tpu_custom_call" | custom-call | tf_op jit(solution)/shard_map/pallas_call | solution.py:208
  11.6 0.6 %copy.7 = bf16[2,2048]{1,0:T(2,128)(2,1)} copy(bf16[2,2048]{1,0:T(2,128)(2,1)S(1)} %shard_map.55) | data formatting | bytes 16384
